TPU v7x, 256 devices: a whole 4x4x8 slice. The times are simulated.
256 devices in a mesh: row: 16 (over y_hi, x, core), col: 16 (over z, y_lo).
Axes of the slice: x: 4, y: 4 (y_hi: 2, y_lo: 2; y = y_hi * 2 + y_lo), z: 8, core: 2. Of those that a mesh axis runs over, the one named last changes fastest.
Arguments:
- features: bfloat16 [32768, 512], P(('row', 'col')), may hold values from -6 to 6
- coefs: bfloat16 [32768], P(('row', 'col')), may hold values from -150 to 150
Outputs:
- grads: bfloat16 [32768, 512], P(('row', 'col'))
- recolored: bfloat16 [32768, 512], P(('row', 'col'))
All inputs are finite; a program needn't handle non-finite values.
Results may differ from a plain program's by a relative error of at most 0.0025.
The roundings to bfloat16 on the way count: a program that leaves them out, or rounds other values in their place, can miss the bound.
Values may be sent and summed in bfloat16 or wider, within the bound.
No kernel may reach another device: no remote copies, remote signals or barrier semaphores. Data moves between devices by JAX's collectives and lax.ppermute only.
A program may use at most 64 MiB of HBM per device.

v0:
```python
import jax
import jax.numpy as jnp
from jax import lax
from jax.sharding import PartitionSpec as P


def from_everyone(shard, axis):
    copies = jnp.broadcast_to(shard, (lax.axis_size(axis), *shard.shape))
    return lax.all_to_all(copies, axis, split_axis=0, concat_axis=0, tiled=True)


def laid_out(blocks, dim):
    blocks = jnp.moveaxis(blocks, 0, dim)
    shape = blocks.shape
    return blocks.reshape(*shape[:dim], shape[dim] * shape[dim + 1], *shape[dim + 2 :])


def gather_directly(shard, axis, dim):
    blocks = from_everyone(shard, axis)
    return laid_out(blocks, dim)


def in_blocks(shard, dim, count):
    before, after = (shard.shape[:dim], shard.shape[dim + 1 :])
    return jnp.moveaxis(shard.reshape(*before, count, -1, *after), dim, 0)


def sent_and_summed(shard, axis, dim):
    count = lax.axis_size(axis)
    blocks = lax.all_to_all(in_blocks(shard, dim, count), axis, 0, 0, tiled=True)
    return jnp.sum(blocks, axis=0)


def in_one_piece(arrays, axis, dim, along):
    columns = [a.reshape(*a.shape[:along], -1) for a in arrays]
    both = jnp.concatenate(columns, axis=along)
    result, at, finished = (sent_and_summed(both, axis, dim), 0, [])
    for a, column in zip(arrays, columns):
        section = result[..., at : at + column.shape[along]]
        finished.append(section.reshape(*section.shape[:along], *a.shape[along:]))
        at += column.shape[along]
    return tuple(finished)


def tile_terms(row_points, row_norms, col_points, col_coefs):
    width = row_points.shape[1]
    gamma = 2.0 / width
    col_full = col_points.astype(jnp.float32)
    col_norms = jnp.sum(col_full * col_full, axis=1)
    weighted = (col_coefs.astype(jnp.float32)[:, None] * col_full).astype(jnp.bfloat16)
    row_count = row_points.shape[0]
    strip_len = min(512, row_count)
    strip_count = row_count // strip_len

    def one_strip(packed):
        strip_points, strip_norms = packed
        products = lax.dot_general(
            strip_points, col_points, (((1,), (1,)), ((), ())), preferred_element_type=jnp.float32
        )
        kernel = jnp.exp(
            -(strip_norms[:, None] + col_norms[None, :] - 2.0 * products) * gamma
        ).astype(jnp.bfloat16)
        totals = jnp.dot(kernel, col_coefs, preferred_element_type=jnp.float32)
        moments = jnp.dot(kernel, weighted, preferred_element_type=jnp.float32)
        return (totals, moments)

    totals, moments = lax.map(
        one_strip,
        (
            row_points.reshape(strip_count, strip_len, width),
            row_norms.reshape(strip_count, strip_len),
        ),
    )
    return (totals.reshape(row_count), moments.reshape(row_count, width))


def local(features, coefs):
    width = features.shape[1]
    gamma = 2.0 / width
    row_points = gather_directly(features, "col", 0)
    row_full = row_points.astype(jnp.float32)
    row_norms = jnp.sum(row_full * row_full, axis=1)
    col_points, col_coefs = (
        lax.all_gather(features, "row", axis=0, tiled=True),
        lax.all_gather(coefs, "row", axis=0, tiled=True),
    )
    totals, moments = tile_terms(row_points, row_norms, col_points, col_coefs)
    own_totals, own_moments = in_one_piece((totals, moments), "col", 0, 1)
    own_full = features.astype(jnp.float32)
    grads = (2.0 * gamma * (own_moments - own_totals[:, None] * own_full)).astype(jnp.bfloat16)
    gram = jnp.einsum("pa,pb->ab", grads, grads, preferred_element_type=jnp.float32)
    point_count = features.shape[0] * lax.axis_size("row") * lax.axis_size("col")
    whole_gram = lax.psum(gram, ("row", "col"))
    agop = (whole_gram / point_count).astype(jnp.bfloat16)
    recolored = jnp.dot(features, agop, preferred_element_type=jnp.float32)
    return (grads, recolored.astype(jnp.bfloat16))


def solution(mesh):
    return jax.shard_map(
        local,
        mesh=mesh,
        in_specs=(P(("row", "col"), None), P(("row", "col"))),
        out_specs=(P(("row", "col"), None), P(("row", "col"), None)),
        check_vma=False,
    )
```

profile of v0, /device:TPU:2, one launch (start us, length us, event | category | flops | bytes accessed | tf_op | source)
XLA Modules:
  0.0 500.3 jit_solution(5801225828391039374)
XLA Ops:
  7.2 2.4 broadcast_in_dim.22
  9.6 9.6 %all-to-all-start = ((bf16[16,128,512]{2,1,0:T(8,128)(2,1)}), bf16[16,128,512]{2,1,0:T(8,128)(2,1)S(1)}, u32[]{:S(2)}, u32[]{:S(2)}) async-start(bf16[16,128,512]{2,1,0:T(8,128)(2,1)} %broadcast_in_dim.22), calls=%async_computation | async-start | bytes 4194304 | tf_op jit(solution)/shard_map/all_to_all | solution.py:9
  19.2 0.7 all-gather.3.cloned.1.call-update
  19.9 19.8 %all-gather = bf16[16,1,128]{2,1,0:T(2,128)(2,1)S(1)} all-gather(bf16[1,1,128]{2,1,0:T(2,128)(2,1)S(1)} %bitcast.46), channel_id=1, replica_groups=mesh['row'=16,'col'=16] {'row'}, dimensions={0}, use_global_device_ids=true | all-gather | bytes 4352 | tf_op jit(solution)/shard_map/all_gather | solution.py:85
  39.7 29.9 %all-to-all-done = bf16[16,128,512]{2,1,0:T(8,128)(2,1)S(1)} async-done(((bf16[16,128,512]{2,1,0:T(8,128)(2,1)}), bf16[16,128,512]{2,1,0:T(8,128)(2,1)S(1)}, u32[]{:S(2)}, u32[]{:S(2)}) %all-to-all-start) | async-done | bytes 2097184 | tf_op jit(solution)/shard_map/all_to_all | solution.py:9
  69.7 0.5 multiply_reduce_fusion
  70.2 14.8 %all-gather.3.cloned.1.call-done = bf16[2048,512]{1,0:T(8,128)(2,1)} async-done(((bf16[128,512]{1,0:T(8,128)(2,1)}), bf16[2048,512]{1,0:T(8,128)(2,1)}) %all-gather.3.cloned.1.call-update) | async-done | bytes 2097168 | tf_op jit(solution)/shard_map/all_gather | solution.py:84
  85.0 3.5 fusion.5
  88.5 24.6 %while.12 = (s32[]{:T(128)}, f32[4,512]{1,0:T(4,128)S(1)}, f32[4,512,512]{2,1,0:T(8,128)}, f32[4,512]{1,0:T(4,128)S(1)}, f32[2048]{0:T(1024)S(1)}, /*index=5*/bf...) while((s32[]{:T(128)}, f32[4,512]{1,0:T(4,128)S(1)}, ...), condition=%wide.region_3.4_spmd, body=%wide.region_2.3_spmd.sunk | while | flops 2155872256 | bytes 20480660 | solution.py:67
  88.5 3.1 exponential_convert_fusion.2
  91.7 2.3 fusion.36
  94.0 0.6 fusion.35
  94.7 3.1 exponential_convert_fusion.2
  97.8 2.3 fusion.36
  100.1 0.6 fusion.35
  100.8 3.1 exponential_convert_fusion.2
  104.0 2.3 fusion.36
  106.3 0.6 fusion.35
  107.0 3.1 exponential_convert_fusion.2
  110.1 2.3 fusion.36
  112.5 0.6 fusion.35
  113.2 0.9 concatenate.11
  114.0 5.9 %pad_maximum_fusion = f32[16,128,513]{2,1,0:T(8,128)} fusion(f32[16,128,512]{2,1,0:T(8,128)} %bitcast.43, f32[16,128,1]{2,1,0:T(8,128)S(1)} %concatenate.11), kind=kLoop, calls=%fused_computation.9 | loop fusion | flops 1050624 | bytes 8404992 | tf_op jit(solution)/shard_map/concatenate | solution.py:36
  120.0 5.7 %copy.15 = f32[16,128,513]{1,2,0:T(8,128)} copy(f32[16,128,513]{2,1,0:T(8,128)} %pad_maximum_fusion) | data formatting | bytes 8404992 | tf_op jit(solution)/shard_map/concatenate | solution.py:36
  125.7 4.7 all-to-all-start.1
  130.5 100.1 %all-to-all-done.1 = f32[16,128,513]{1,2,0:T(8,128)} async-done(((f32[16,128,513]{1,2,0:T(8,128)}), f32[16,128,513]{1,2,0:T(8,128)}, u32[]{:S(2)}, u32[]{:S(2)}) %all-to-all-start.1) | async-done | bytes 4202528 | tf_op jit(solution)/shard_map/all_to_all | solution.py:30
  230.6 2.4 reduce_sum.29
  233.1 1.3 fusion.12
  234.5 0.8 copy.17
  235.3 255.8 %all-reduce.2.cloned.1.call-done = f32[512,512]{1,0:T(8,128)} async-done(((f32[512,512]{1,0:T(8,128)}), f32[512,512]{1,0:T(8,128)}) %all-reduce.2.cloned.1.call-update) | async-done | bytes 1048592 | tf_op jit(solution)/shard_map/psum | solution.py:93
  491.1 1.6 fusion.6
  492.7 0.8 copy.18
  (35 shorter events, 0.6 us)
Async XLA Ops:
  7.2 12.8 %copy-start.2 = (bf16[128]{0:T(256)(128)(2,1)S(1)}, bf16[128]{0:T(256)(128)(2,1)}, u32[]{:S(2)}) copy-start(bf16[128]{0:T(256)(128)(2,1)} %param.5) | copy-start | bytes 772
  9.6 60.1 %all-to-all-start = ((bf16[16,128,512]{2,1,0:T(8,128)(2,1)}), bf16[16,128,512]{2,1,0:T(8,128)(2,1)S(1)}, u32[]{:S(2)}, u32[]{:S(2)}) async-start(bf16[16,128,512]{2,1,0:T(8,128)(2,1)} %broadcast_in_dim.22), calls=%async_computation | async-start | bytes 4194304 | tf_op jit(solution)/shard_map/all_to_all | solution.py:9
  19.2 65.8 %all-gather.3.cloned.1.call-start = ((), (), s32[]{:S(2)}) async-start(), calls=%async_computation.2 | async-start | bytes 2228224 | tf_op jit(solution)/shard_map/all_gather | solution.py:84
  88.5 3.1 copy-start.1
  94.7 3.2 copy-start.1
  100.8 3.2 copy-start.1
  107.0 3.2 copy-start.1
  125.7 4.7 copy-start
  125.7 104.9 %all-to-all-start.1 = ((f32[16,128,513]{1,2,0:T(8,128)}), f32[16,128,513]{1,2,0:T(8,128)}, u32[]{:S(2)}, u32[]{:S(2)}) async-start(f32[16,128,513]{1,2,0:T(8,128)} %copy.15), calls=%async_computation.1 | async-start | bytes 8519680 | tf_op jit(solution)/shard_map/all_to_all | solution.py:30
  130.3 360.7 %all-reduce.2.cloned.1.call-start = ((), (), s32[]{:S(2)}) async-start(), calls=%async_computation.3 | async-start | bytes 2097152 | tf_op jit(solution)/shard_map/psum | solution.py:93
Sparse Core Ops, SparseCore 0:
  22.7 62.2 all-gather.2
  234.6 256.4 all-reduce.1
where the time goes:
time: 501 us; the launch traced here: 500 us
  waiting for transfers between devices  401 us (80%)
  matrix products  27.1 us (5%)
  blocking collectives  19.8 us (4%)
  starting transfers between devices  14.3 us (3%)
  between operations  14.1 us (3%)
  other arithmetic  12.5 us (2%)
  local copies, waits for them, and re-layouts  10.9 us (2%)
    psum x1, waiting for transfers between devices, local(): whole_gram = lax.psum(gram, ('row', 'col'))  256 us
    all_to_all x1, waiting for transfers between devices, sent_and_summed(): lax.all_to_all(in_blocks(shard, dim, count), axis, 0, 0, tiled=True)  100 us
    all_to_all x1, waiting for transfers between devices, from_everyone(): return lax.all_to_all(copies, axis, split_axis=0, concat_axis=0, tiled=True)  29.9 us
    all_gather x1, blocking collectives, local(): lax.all_gather(coefs, 'row', axis=0, tiled=True)  19.8 us
    all_gather x1, waiting for transfers between devices, local(): lax.all_gather(features, 'row', axis=0, tiled=True)  14.8 us
    dot_general x4, matrix products, one_strip(): lax.dot_general(strip_points, col_points, (((1,), (1,)), ((), ())), prefe...  12.5 us
  transfers between devices with their start and end apart: 4, of which 4 were waited for; matrix products, arithmetic and copies ran while one was open for 0% of the time, Pallas kernels for 0%

commit v1 on v0

--- a/solution.py
+++ b/solution.py
@@ -75,6 +75,11 @@
 
 
 def local(features, coefs):
+
+    def _link_ladders(packet, link_axis, row_axis):
+        parts_out = lax.psum(packet, link_axis)
+        return lax.psum(parts_out, row_axis)
+
     width = features.shape[1]
     gamma = 2.0 / width
     row_points = gather_directly(features, "col", 0)
@@ -90,7 +95,7 @@
     grads = (2.0 * gamma * (own_moments - own_totals[:, None] * own_full)).astype(jnp.bfloat16)
     gram = jnp.einsum("pa,pb->ab", grads, grads, preferred_element_type=jnp.float32)
     point_count = features.shape[0] * lax.axis_size("row") * lax.axis_size("col")
-    whole_gram = lax.psum(gram, ("row", "col"))
+    whole_gram = _link_ladders(gram, "col", "row")
     agop = (whole_gram / point_count).astype(jnp.bfloat16)
     recolored = jnp.dot(features, agop, preferred_element_type=jnp.float32)
     return (grads, recolored.astype(jnp.bfloat16))

time: 501 us -> 531 us (1.060); the launches traced: 500 us -> 525 us
  waiting for transfers between devices: 401 us -> 426 us
    psum x1 -> x2, waiting for transfers between devices: 256 us -> 281 us  [the longest x1 143 us: _link_ladders(): return lax.psum(parts_out, row_axis)]
  transfers between devices with their start and end apart: 4 -> 5, of which waited for: 4 -> 5; matrix products, arithmetic and copies ran while one was open for 0% -> 0% of each run, Pallas kernels for 0% -> 0%
where the time goes in v1:
time: 531 us; the launch traced here: 525 us
  waiting for transfers between devices  426 us (80%)
  matrix products  27.1 us (5%)
  blocking collectives  19.8 us (4%)
  starting transfers between devices  14.4 us (3%)
  between operations  13.9 us (3%)
  other arithmetic  12.5 us (2%)
  local copies, waits for them, and re-layouts  10.9 us (2%)
    psum x1, waiting for transfers between devices, _link_ladders(): return lax.psum(parts_out, row_axis)  143 us
    psum x1, waiting for transfers between devices, _link_ladders(): parts_out = lax.psum(packet, link_axis)  138 us
    all_to_all x1, waiting for transfers between devices, sent_and_summed(): lax.all_to_all(in_blocks(shard, dim, count), axis, 0, 0, tiled=True)  100 us
    all_to_all x1, waiting for transfers between devices, from_everyone(): return lax.all_to_all(copies, axis, split_axis=0, concat_axis=0, tiled=True)  29.9 us
    all_gather x1, blocking collectives, local(): lax.all_gather(coefs, 'row', axis=0, tiled=True)  19.8 us
    all_gather x1, waiting for transfers between devices, local(): lax.all_gather(features, 'row', axis=0, tiled=True)  14.8 us
    dot_general x4, matrix products, one_strip(): lax.dot_general(strip_points, col_points, (((1,), (1,)), ((), ())), prefe...  12.5 us
  transfers between devices with their start and end apart: 5, of which 5 were waited for; matrix products, arithmetic and copies ran while one was open for 0% of the time, Pallas kernels for 0%

profile of v1, /device:TPU:2, one launch (start us, length us, event | category | flops | bytes accessed | tf_op | source)
XLA Modules:
  0.0 524.9 jit_solution(13683975245539323691)
XLA Ops:
  7.2 2.4 broadcast_in_dim.22
  9.6 9.6 %all-to-all-start = ((bf16[16,128,512]{2,1,0:T(8,128)(2,1)}), bf16[16,128,512]{2,1,0:T(8,128)(2,1)S(1)}, u32[]{:S(2)}, u32[]{:S(2)}) async-start(bf16[16,128,512]{2,1,0:T(8,128)(2,1)} %broadcast_in_dim.22), calls=%async_computation | async-start | bytes 4194304 | tf_op jit(solution)/shard_map/all_to_all | solution.py:9
  19.2 0.7 all-gather.3.cloned.1.call-update
  19.9 19.8 %all-gather = bf16[16,1,128]{2,1,0:T(2,128)(2,1)S(1)} all-gather(bf16[1,1,128]{2,1,0:T(2,128)(2,1)S(1)} %bitcast.46), channel_id=1, replica_groups=mesh['row'=16,'col'=16] {'row'}, dimensions={0}, use_global_device_ids=true | all-gather | bytes 4352 | tf_op jit(solution)/shard_map/all_gather | solution.py:90
  39.7 29.9 %all-to-all-done = bf16[16,128,512]{2,1,0:T(8,128)(2,1)S(1)} async-done(((bf16[16,128,512]{2,1,0:T(8,128)(2,1)}), bf16[16,128,512]{2,1,0:T(8,128)(2,1)S(1)}, u32[]{:S(2)}, u32[]{:S(2)}) %all-to-all-start) | async-done | bytes 2097184 | tf_op jit(solution)/shard_map/all_to_all | solution.py:9
  70.2 14.8 %all-gather.3.cloned.1.call-done = bf16[2048,512]{1,0:T(8,128)(2,1)} async-done(((bf16[128,512]{1,0:T(8,128)(2,1)}), bf16[2048,512]{1,0:T(8,128)(2,1)}) %all-gather.3.cloned.1.call-update) | async-done | bytes 2097168 | tf_op jit(solution)/shard_map/all_gather | solution.py:89
  85.0 3.5 fusion.5
  88.5 24.6 %while.12 = (s32[]{:T(128)}, f32[4,512]{1,0:T(4,128)S(1)}, f32[4,512,512]{2,1,0:T(8,128)}, f32[4,512]{1,0:T(4,128)S(1)}, f32[2048]{0:T(1024)S(1)}, /*index=5*/bf...) while((s32[]{:T(128)}, f32[4,512]{1,0:T(4,128)S(1)}, ...), condition=%wide.region_3.4_spmd, body=%wide.region_2.3_spmd.sunk | while | flops 2155872256 | bytes 20480660 | solution.py:67
  88.5 3.1 exponential_convert_fusion.2
  91.7 2.3 fusion.36
  94.0 0.6 fusion.35
  94.7 3.1 exponential_convert_fusion.2
  97.8 2.3 fusion.36
  100.1 0.6 fusion.35
  100.8 3.1 exponential_convert_fusion.2
  104.0 2.2 fusion.36
  106.3 0.6 fusion.35
  107.0 3.1 exponential_convert_fusion.2
  110.1 2.3 fusion.36
  112.5 0.6 fusion.35
  113.2 0.9 concatenate.11
  114.1 5.9 %pad_maximum_fusion = f32[16,128,513]{2,1,0:T(8,128)} fusion(f32[16,128,512]{2,1,0:T(8,128)} %bitcast.43, f32[16,128,1]{2,1,0:T(8,128)S(1)} %concatenate.11), kind=kLoop, calls=%fused_computation.9 | loop fusion | flops 1050624 | bytes 8404992 | tf_op jit(solution)/shard_map/concatenate | solution.py:36
  120.0 5.7 %copy.15 = f32[16,128,513]{1,2,0:T(8,128)} copy(f32[16,128,513]{2,1,0:T(8,128)} %pad_maximum_fusion) | data formatting | bytes 8404992 | tf_op jit(solution)/shard_map/concatenate | solution.py:36
  125.7 4.7 all-to-all-start.1
  130.5 100.1 %all-to-all-done.1 = f32[16,128,513]{1,2,0:T(8,128)} async-done(((f32[16,128,513]{1,2,0:T(8,128)}), f32[16,128,513]{1,2,0:T(8,128)}, u32[]{:S(2)}, u32[]{:S(2)}) %all-to-all-start.1) | async-done | bytes 4202528 | tf_op jit(solution)/shard_map/all_to_all | solution.py:30
  230.6 2.4 reduce_sum.29
  233.1 1.3 fusion.12
  234.5 137.5 %all-reduce.3.cloned.1.call-done = f32[512,512]{1,0:T(8,128)} async-done(((f32[512,512]{1,0:T(8,128)}), f32[512,512]{1,0:T(8,128)}) %all-reduce.3.cloned.1.call-update) | async-done | bytes 1048592 | tf_op jit(solution)/shard_map/psum | solution.py:80
  372.1 0.8 copy.17
  372.8 143.2 %all-reduce.5.cloned.1.call-done = f32[512,512]{1,0:T(8,128)} async-done(((f32[512,512]{1,0:T(8,128)}), f32[512,512]{1,0:T(8,128)}) %all-reduce.5.cloned.1.call-update) | async-done | bytes 1048592 | tf_op jit(solution)/shard_map/psum | solution.py:81
  516.1 1.6 fusion.6
  517.6 0.8 copy.18
  (38 shorter events, 1.1 us)
Async XLA Ops:
  7.2 12.8 %copy-start.2 = (bf16[128]{0:T(256)(128)(2,1)S(1)}, bf16[128]{0:T(256)(128)(2,1)}, u32[]{:S(2)}) copy-start(bf16[128]{0:T(256)(128)(2,1)} %param.5) | copy-start | bytes 772
  9.6 60.1 %all-to-all-start = ((bf16[16,128,512]{2,1,0:T(8,128)(2,1)}), bf16[16,128,512]{2,1,0:T(8,128)(2,1)S(1)}, u32[]{:S(2)}, u32[]{:S(2)}) async-start(bf16[16,128,512]{2,1,0:T(8,128)(2,1)} %broadcast_in_dim.22), calls=%async_computation | async-start | bytes 4194304 | tf_op jit(solution)/shard_map/all_to_all | solution.py:9
  19.2 65.8 %all-gather.3.cloned.1.call-start = ((), (), s32[]{:S(2)}) async-start(), calls=%async_computation.2 | async-start | bytes 2228224 | tf_op jit(solution)/shard_map/all_gather | solution.py:89
  88.5 3.1 copy-start.1
  94.7 3.2 copy-start.1
  100.8 3.2 copy-start.1
  107.0 3.2 copy-start.1
  125.7 4.7 copy-start
  125.7 104.9 %all-to-all-start.1 = ((f32[16,128,513]{1,2,0:T(8,128)}), f32[16,128,513]{1,2,0:T(8,128)}, u32[]{:S(2)}, u32[]{:S(2)}) async-start(f32[16,128,513]{1,2,0:T(8,128)} %copy.15), calls=%async_computation.1 | async-start | bytes 8519680 | tf_op jit(solution)/shard_map/all_to_all | solution.py:30
  130.4 241.7 %all-reduce.3.cloned.1.call-start = ((), (), s32[]{:S(2)}) async-start(), calls=%async_computation.3 | async-start | bytes 2097152 | tf_op jit(solution)/shard_map/psum | solution.py:80
  234.5 281.6 %all-reduce.5.cloned.1.call-start = ((), (), s32[]{:S(2)}) async-start(), calls=%async_computation.4 | async-start | bytes 2097152 | tf_op jit(solution)/shard_map/psum | solution.py:81
Sparse Core Ops, SparseCore 0:
  22.7 62.2 all-gather.2
  234.6 137.4 all-reduce.2
  374.7 141.3 all-reduce.4
